TPU v7x, 512 devices: a whole 4x4x16 slice. The times are simulated.
512 devices in a mesh: rows: 64 (over x, y, z_hi, core), cols: 8 (over z_lo).
Axes of the slice: x: 4, y: 4, z: 16 (z_hi: 2, z_lo: 8; z = z_hi * 8 + z_lo), core: 2. Of those that a mesh axis runs over, the one named last changes fastest.
Arguments:
- homolog_embedding: bfloat16 [512, 1024, 256], P('rows', 'cols'), may hold values from -120 to 120
- couple_embedding: bfloat16 [1024, 1024, 128], P('rows', 'cols'), may hold values from -6 to 6
- homolog_standardize_factor: float32 [256], replicated, may hold values from 0.25 to 1.75
- first_factor_mapping: bfloat16 [256, 32], replicated, may hold values from -0.375 to 0.375
- second_factor_mapping: bfloat16 [256, 32], replicated, may hold values from -0.375 to 0.375
- contraction_to_couple_mapping: bfloat16 [1024, 128], replicated, may hold values from -4 to 4
- couple_standardize_factor: float32 [128], replicated, may hold values from 0.25 to 1.75
- widening_matrix: bfloat16 [128, 512], replicated, may hold values from -0.5 to 0.5
- narrowing_matrix: bfloat16 [512, 128], replicated, may hold values from -0.25 to 0.25
Outputs:
- pair_out: bfloat16 [1024, 1024, 128], P('rows', 'cols')
All inputs are finite; a program needn't handle non-finite values.
Results may differ from a plain program's by a relative error of at most 0.0064.
Values may be sent and summed in bfloat16 or wider, within the bound.
A program may use at most 64 MiB of HBM per device.

v0:
```python
import math
import jax
import jax.numpy as jnp
from jax import lax
from jax.sharding import PartitionSpec as P


def standardize_features(sampled_entries, gain_vector):
    floats = sampled_entries.astype(jnp.float32)
    average = jnp.mean(floats, axis=-1, keepdims=True)
    centred = floats - average
    variance = jnp.mean(centred * centred, axis=-1, keepdims=True)
    return centred * lax.rsqrt(variance + 1e-05) * gain_vector


def project_rows(sampled_entries, weights):
    unrolled_tensor = sampled_entries.reshape(-1, sampled_entries.shape[2])
    product = jnp.dot(unrolled_tensor, weights, preferred_element_type=jnp.float32).astype(
        jnp.bfloat16
    )
    return product.reshape(sampled_entries.shape[0], sampled_entries.shape[1], weights.shape[1])


def on_device(
    homolog_embedding,
    couple_embedding,
    homolog_standardize_factor,
    first_factor_mapping,
    second_factor_mapping,
    contraction_to_couple_mapping,
    couple_standardize_factor,
    widening_matrix,
    narrowing_matrix,
):
    standardized_tensor = standardize_features(
        homolog_embedding, homolog_standardize_factor
    ).astype(jnp.bfloat16)
    res_local = standardized_tensor.shape[1]
    width_outer = first_factor_mapping.shape[1]
    right_local = project_rows(standardized_tensor, second_factor_mapping)
    left_local = project_rows(standardized_tensor, first_factor_mapping)
    copies = jnp.tile(left_local, (1, lax.axis_size("cols"), 1))
    left_tile = lax.all_to_all(
        lax.all_to_all(copies, "cols", split_axis=1, concat_axis=1, tiled=True),
        "rows",
        split_axis=1,
        concat_axis=0,
        tiled=True,
    )
    right_panel = lax.all_gather(right_local, "rows", axis=0, tiled=True)
    sequences = left_tile.shape[0]
    tile_height = left_tile.shape[1]
    block = math.gcd(tile_height, 4)
    block_count = tile_height // block
    left_blocks = left_tile.reshape(sequences, block_count, block * width_outer).transpose(1, 0, 2)
    right_matrix = right_panel.reshape(sequences, res_local * width_outer)

    def project_block(left_block):
        outer_product = (
            lax.dot_general(
                left_block,
                right_matrix,
                (((0,), (0,)), ((), ())),
                preferred_element_type=jnp.float32,
            )
            / sequences
        )
        outer_product = outer_product.astype(jnp.bfloat16).reshape(
            block, width_outer, res_local, width_outer
        )
        outer_product = outer_product.transpose(0, 2, 1, 3).reshape(
            block * res_local, width_outer * width_outer
        )
        return jnp.dot(
            outer_product, contraction_to_couple_mapping, preferred_element_type=jnp.float32
        )

    update = lax.map(project_block, left_blocks).reshape(
        tile_height, res_local, contraction_to_couple_mapping.shape[1]
    )
    pair_mid = couple_embedding.astype(jnp.float32) + update
    pair_normed = (
        standardize_features(pair_mid, couple_standardize_factor)
        .astype(jnp.bfloat16)
        .reshape(-1, couple_embedding.shape[2])
    )
    hidden = jnp.maximum(
        jnp.dot(pair_normed, widening_matrix, preferred_element_type=jnp.float32), 0.0
    ).astype(jnp.bfloat16)
    result = pair_mid + jnp.dot(
        hidden, narrowing_matrix, preferred_element_type=jnp.float32
    ).reshape(couple_embedding.shape)
    return result.astype(jnp.bfloat16)


def solution(mesh):
    return jax.shard_map(
        on_device,
        mesh=mesh,
        in_specs=(
            P("rows", "cols", None),
            P("rows", "cols", None),
            P(),
            P(),
            P(),
            P(),
            P(),
            P(),
            P(),
        ),
        out_specs=P("rows", "cols", None),
        check_vma=False,
    )
```

profile of v0, /device:TPU:1, one launch (start us, length us, event | category | flops | bytes accessed | tf_op | source)
XLA Modules:
  0.0 234.6 jit_solution(8320753588659107767)
XLA Ops:
  6.5 0.0 copy-start
  6.5 1.3 convert_reduce_fusion
  7.9 1.4 fusion.12
  9.3 1.4 fusion.14
  10.7 0.2 fusion.11
  10.9 0.7 copy.40
  11.6 0.0 all-gather.2.cloned.1.call-update
  11.6 0.2 fusion.10
  11.9 0.2 copy.24
  12.1 0.3 tile.11
  12.4 2.0 reshape.66
  14.4 39.6 %all_to_all.20 = bf16[8,2,16384]{2,1,0:T(2,128)(2,1)S(1)} all-to-all(bf16[8,2,16384]{2,1,0:T(2,128)(2,1)S(1)} %reshape.66), channel_id=1, replica_groups=mesh['rows'=64,'cols'=8] {'cols'}, dimensions={0} | all-to-all | bytes 1048576 | tf_op jit(solution)/shard_map/all_to_all | solution.py:44
  53.9 1.0 reshape.67
  55.0 1.5 bitcast_bitcast_fusion
  56.4 4.5 %reshape.68 = bf16[64,2,2048]{2,1,0:T(2,128)(2,1)} reshape(bf16[1024,8,32]{2,1,0:T(8,128)(2,1)} %bitcast_bitcast_fusion) | data formatting | bytes 1048576
  60.9 18.2 %all-to-all-start.1 = ((bf16[64,2,2048]{2,1,0:T(2,128)(2,1)}), bf16[64,2,2048]{2,1,0:T(2,128)(2,1)}, u32[]{:S(2)}, u32[]{:S(2)}) async-start(bf16[64,2,2048]{2,1,0:T(2,128)(2,1)} %reshape.68), calls=%async_computation.1 | async-start | bytes 1048576 | tf_op jit(solution)/shard_map/all_to_all | solution.py:43
  79.1 35.0 %all-to-all-done.1 = bf16[64,2,2048]{2,1,0:T(2,128)(2,1)} async-done(((bf16[64,2,2048]{2,1,0:T(2,128)(2,1)}), bf16[64,2,2048]{2,1,0:T(2,128)(2,1)}, u32[]{:S(2)}, u32[]{:S(2)}) %all-to-all-start.1) | async-done | bytes 524320 | tf_op jit(solution)/shard_map/all_to_all | solution.py:43
  114.1 3.0 %reshape.69 = bf16[1024,8,32]{2,1,0:T(8,128)(2,1)S(1)} reshape(bf16[64,2,2048]{2,1,0:T(2,128)(2,1)} %all-to-all-done.1) | data formatting | bytes 1048576
  117.2 1.9 copy.26
  119.1 3.1 %reshape.60 = bf16[512,4,128]{2,1,0:T(4,128)(2,1)S(1)} reshape(bf16[64,8,16,32]{3,2,1,0:T(8,128)(2,1)} %copy.26) | data formatting | bytes 1048576 | tf_op jit(solution)/shard_map/reshape | solution.py:55
  122.2 0.1 copy.29
  122.3 40.2 %all-gather.2.cloned.1.call-done = bf16[512,128,32]{1,2,0:T(8,128)(2,1)} async-done(((bf16[8,128,32]{1,2,0:T(8,128)(2,1)}), bf16[512,128,32]{1,2,0:T(8,128)(2,1)}) %all-gather.2.cloned.1.call-update) | async-done | bytes 4194320 | tf_op jit(solution)/shard_map/all_gather | solution.py:50
  162.5 8.6 %copy.28 = bf16[512,128,32]{0,2,1:T(8,128)(2,1)} copy(bf16[512,128,32]{1,2,0:T(8,128)(2,1)} %all-gather.2.cloned.1.call-done) | data formatting | bytes 8388608 | tf_op jit(solution)/shard_map/all_gather | solution.py:50
  171.1 6.4 %copy.30 = bf16[512,4096]{1,0:T(8,128)(2,1)} copy(bf16[512,4096]{0,1:T(8,128)(2,1)} %bitcast.72) | data formatting | bytes 8388608 | tf_op jit(solution)/shard_map/while | solution.py:78
  177.5 46.2 %while.10 = (s32[]{:T(128)}, f32[4,512,128]{2,1,0:T(8,128)S(1)}, bf16[4,512,128]{2,1,0:T(8,128)(2,1)S(1)}, bf16[512,4096]{1,0:T(8,128)(2,1)}, bf16[1024,128]{1,0:T(8,128)(2,1)S(1)}, /*index=5*/s32[]{:T(128)}) while((s32[]{:T(128)}, f32[4,512,128]{2,1,0:T(8,128)S(1)}, bf16[4,512,128]{2,1,0:T(8,128)(2,1)S(1)}, bf16[512,4096]{1,0:T(8,128)(2,1)}, ...), condition=%wide.region_3.4_spmd, body=%wide.region_2.3_spmd.sunk | while | flops 672137216 | bytes 11141197 | solution.py:78
  177.5 3.0 %fusion.36 = bf16[128,4096]{1,0:T(8,128)(2,1)S(1)} fusion(bf16[512,4096]{1,0:T(8,128)(2,1)} %get-tuple-element.104, bf16[4,512,128]{2,1,0:T(8,128)(2,1)S(1)} %get-tuple-element.103, s32[]{:T(128)} %get-tuple-element.95), kind=kOutput, calls=%fused_computation.1.clone.1 | convolution fusion | flops 537919488 | bytes 5373956 | tf_op jit(solution)/shard_map/while/body/eval_jaxpr/dot_general | solution.py:60
  180.5 4.4 %reshape.71 = bf16[4,32,128,32]{3,2,1,0:T(8,128)(2,1)} reshape(bf16[128,4096]{1,0:T(8,128)(2,1)S(1)} %fusion.36) | data formatting | bytes 2097152 | tf_op jit(solution)/shard_map/while/body/eval_jaxpr/reshape | solution.py:68
  184.9 3.7 %copy.44 = bf16[4,128,32,32]{1,0,3,2:T(4,128)(2,1)S(1)} copy(bf16[4,128,32,32]{3,1,2,0:T(8,128)(2,1)} %bitcast.66) | data formatting | bytes 2097152 | tf_op jit(solution)/shard_map/while/body/eval_jaxpr/transpose | solution.py:71
  188.6 0.5 fusion.37
  189.1 2.9 %fusion.36 = bf16[128,4096]{1,0:T(8,128)(2,1)S(1)} fusion(bf16[512,4096]{1,0:T(8,128)(2,1)} %get-tuple-element.104, bf16[4,512,128]{2,1,0:T(8,128)(2,1)S(1)} %get-tuple-element.103, s32[]{:T(128)} %get-tuple-element.95), kind=kOutput, calls=%fused_computation.1.clone.1 | convolution fusion | flops 537919488 | bytes 5373956 | tf_op jit(solution)/shard_map/while/body/eval_jaxpr/dot_general | solution.py:60
  192.1 4.4 %reshape.71 = bf16[4,32,128,32]{3,2,1,0:T(8,128)(2,1)} reshape(bf16[128,4096]{1,0:T(8,128)(2,1)S(1)} %fusion.36) | data formatting | bytes 2097152 | tf_op jit(solution)/shard_map/while/body/eval_jaxpr/reshape | solution.py:68
  196.5 3.7 %copy.44 = bf16[4,128,32,32]{1,0,3,2:T(4,128)(2,1)S(1)} copy(bf16[4,128,32,32]{3,1,2,0:T(8,128)(2,1)} %bitcast.66) | data formatting | bytes 2097152 | tf_op jit(solution)/shard_map/while/body/eval_jaxpr/transpose | solution.py:71
  200.1 0.5 fusion.37
  200.7 2.9 %fusion.36 = bf16[128,4096]{1,0:T(8,128)(2,1)S(1)} fusion(bf16[512,4096]{1,0:T(8,128)(2,1)} %get-tuple-element.104, bf16[4,512,128]{2,1,0:T(8,128)(2,1)S(1)} %get-tuple-element.103, s32[]{:T(128)} %get-tuple-element.95), kind=kOutput, calls=%fused_computation.1.clone.1 | convolution fusion | flops 537919488 | bytes 5373956 | tf_op jit(solution)/shard_map/while/body/eval_jaxpr/dot_general | solution.py:60
  203.6 4.4 %reshape.71 = bf16[4,32,128,32]{3,2,1,0:T(8,128)(2,1)} reshape(bf16[128,4096]{1,0:T(8,128)(2,1)S(1)} %fusion.36) | data formatting | bytes 2097152 | tf_op jit(solution)/shard_map/while/body/eval_jaxpr/reshape | solution.py:68
  208.0 3.7 %copy.44 = bf16[4,128,32,32]{1,0,3,2:T(4,128)(2,1)S(1)} copy(bf16[4,128,32,32]{3,1,2,0:T(8,128)(2,1)} %bitcast.66) | data formatting | bytes 2097152 | tf_op jit(solution)/shard_map/while/body/eval_jaxpr/transpose | solution.py:71
  211.7 0.5 fusion.37
  212.2 2.9 %fusion.36 = bf16[128,4096]{1,0:T(8,128)(2,1)S(1)} fusion(bf16[512,4096]{1,0:T(8,128)(2,1)} %get-tuple-element.104, bf16[4,512,128]{2,1,0:T(8,128)(2,1)S(1)} %get-tuple-element.103, s32[]{:T(128)} %get-tuple-element.95), kind=kOutput, calls=%fused_computation.1.clone.1 | convolution fusion | flops 537919488 | bytes 5373956 | tf_op jit(solution)/shard_map/while/body/eval_jaxpr/dot_general | solution.py:60
  215.1 4.4 %reshape.71 = bf16[4,32,128,32]{3,2,1,0:T(8,128)(2,1)} reshape(bf16[128,4096]{1,0:T(8,128)(2,1)S(1)} %fusion.36) | data formatting | bytes 2097152 | tf_op jit(solution)/shard_map/while/body/eval_jaxpr/reshape | solution.py:68
  219.6 3.7 %copy.44 = bf16[4,128,32,32]{1,0,3,2:T(4,128)(2,1)S(1)} copy(bf16[4,128,32,32]{3,1,2,0:T(8,128)(2,1)} %bitcast.66) | data formatting | bytes 2097152 | tf_op jit(solution)/shard_map/while/body/eval_jaxpr/transpose | solution.py:71
  223.2 0.5 fusion.37
  223.7 0.0 copy-start.4
  223.8 0.3 fusion.15
  224.1 0.0 copy-start.6
  224.1 0.7 multiply_reduce_fusion
  224.8 0.7 multiply_convert_fusion
  225.6 1.2 fusion.7
  226.8 1.0 add_convert_fusion
  (18 shorter events, 0.1 us)
Async XLA Ops:
  6.5 219.0 %copy-start = (bf16[512,128]{1,0:T(8,128)(2,1)S(1)}, bf16[512,128]{1,0:T(8,128)(2,1)}, u32[]{:S(2)}) copy-start(bf16[512,128]{1,0:T(8,128)(2,1)} %param.19) | copy-start | bytes 393220
  6.5 4.1 %copy-start.2 = (bf16[256,32]{0,1:T(8,128)(2,1)S(1)}, bf16[256,32]{0,1:T(8,128)(2,1)}, u32[]{:S(2)}) copy-start(bf16[256,32]{0,1:T(8,128)(2,1)} %param.15) | copy-start | bytes 49156
  6.5 5.1 %copy-start.3 = (bf16[256,32]{0,1:T(8,128)(2,1)S(1)}, bf16[256,32]{0,1:T(8,128)(2,1)}, u32[]{:S(2)}) copy-start(bf16[256,32]{0,1:T(8,128)(2,1)} %param.14) | copy-start | bytes 49156
  6.5 155.9 %all-gather.2.cloned.1.call-start = ((), (), s32[]{:S(2)}) async-start(), calls=%async_computation.2 | async-start | bytes 4259840 | tf_op jit(solution)/shard_map/all_gather | solution.py:50
  60.9 53.3 %all-to-all-start.1 = ((bf16[64,2,2048]{2,1,0:T(2,128)(2,1)}), bf16[64,2,2048]{2,1,0:T(2,128)(2,1)}, u32[]{:S(2)}, u32[]{:S(2)}) async-start(bf16[64,2,2048]{2,1,0:T(2,128)(2,1)} %reshape.68), calls=%async_computation.1 | async-start | bytes 1048576 | tf_op jit(solution)/shard_map/all_to_all | solution.py:43
  171.1 6.4 %copy-start.5 = (bf16[1024,128]{1,0:T(8,128)(2,1)S(1)}, bf16[1024,128]{1,0:T(8,128)(2,1)}, u32[]{:S(2)}) copy-start(bf16[1024,128]{1,0:T(8,128)(2,1)} %param.16) | copy-start | bytes 786436
  177.5 46.2 %copy-start.1 = (bf16[16,128,128]{2,1,0:T(8,128)(2,1)S(1)}, bf16[16,128,128]{2,1,0:T(8,128)(2,1)}, u32[]{:S(2)}) copy-start(bf16[16,128,128]{2,1,0:T(8,128)(2,1)} %param.12) | copy-start | bytes 1572868
  223.7 1.1 copy-start.4
  224.1 1.4 copy-start.6
Sparse Core Ops, SparseCore 0:
  11.7 150.7 all-gather.1
where the time goes:
time: 236 us; the launch traced here: 235 us
  waiting for transfers between devices  75.2 us (32%)
  local copies, waits for them, and re-layouts  65.6 us (28%)
  blocking collectives  39.6 us (17%)
  starting transfers between devices  18.3 us (8%)
  matrix products  15.5 us (7%)
  between operations  13.6 us (6%)
  other arithmetic  6.79 us (3%)
    all_gather x1, waiting for transfers between devices, on_device(): right_panel = lax.all_gather(right_local, 'rows', axis=0, tiled=True)  40.2 us
    all_to_all x1, blocking collectives, on_device(): lax.all_to_all(copies, 'cols', split_axis=1, concat_axis=1, tiled=True)  39.6 us
    all_to_all x1, waiting for transfers between devices, on_device(): lax.all_to_all(lax.all_to_all(copies, 'cols', split_axis=1, concat_axis=1...  35 us
    all_to_all x1, starting transfers between devices, on_device(): lax.all_to_all(lax.all_to_all(copies, 'cols', split_axis=1, concat_axis=1...  18.2 us
    reshape x4, local copies, waits for them, and re-layouts, project_block(): outer_product.astype(jnp.bfloat16)  17.7 us
    transpose x4, local copies, waits for them, and re-layouts, project_block(): outer_product.transpose(0, 2, 1, 3)  14.6 us
    unnamed x20, local copies, waits for them, and re-layouts  12 us
    dot_general x4, matrix products, project_block(): lax.dot_general(left_block, right_matrix, (((0,), (0,)), ((), ())), prefe...  11.8 us
  transfers between devices with their start and end apart: 2, of which 2 were waited for; matrix products, arithmetic and copies ran while one was open for 8% of the time, Pallas kernels for 0%

commit v1 on v0

--- a/solution.py
+++ b/solution.py
@@ -47,7 +47,9 @@
         concat_axis=0,
         tiled=True,
     )
-    right_panel = lax.all_gather(right_local, "rows", axis=0, tiled=True)
+    right_panel = jnp.concatenate(
+        lax.all_to_all(jnp.stack([right_local] * lax.axis_size("rows")), "rows", 0, 0), axis=0
+    )
     sequences = left_tile.shape[0]
     tile_height = left_tile.shape[1]
     block = math.gcd(tile_height, 4)

time: 236 us -> 387 us (1.64)
  the two profiles are of different devices: /device:TPU:1 before, /device:TPU:33 now
where the time goes in v1:
time: 387 us; the launch traced here: 386 us
  waiting for transfers between devices  212 us (55%)
  local copies, waits for them, and re-layouts  91.2 us (24%)
  blocking collectives  38 us (10%)
  starting transfers between devices  20.9 us (5%)
  matrix products  16.2 us (4%)
  other arithmetic  6.79 us (2%)
    all_to_all x1, waiting for transfers between devices, on_device(): lax.all_to_all(jnp.stack([right_local] * lax.axis_size('rows')), 'rows',...  175 us
    all_to_all x1, blocking collectives, on_device(): lax.all_to_all(copies, 'cols', split_axis=1, concat_axis=1, tiled=True)  38 us
    all_to_all x1, waiting for transfers between devices, on_device(): lax.all_to_all(lax.all_to_all(copies, 'cols', split_axis=1, concat_axis=1...  37.2 us
    another operation x1, local copies, waits for them, and re-layouts, on_device(): right_matrix = right_panel.reshape(sequences, res_local * width_outer)  21.7 us
    reshape x4, local copies, waits for them, and re-layouts, project_block(): outer_product.astype(jnp.bfloat16)  17.8 us
    all_to_all x1, starting transfers between devices, on_device(): lax.all_to_all(lax.all_to_all(copies, 'cols', split_axis=1, concat_axis=1...  15.4 us
    transpose x4, local copies, waits for them, and re-layouts, project_block(): outer_product.transpose(0, 2, 1, 3)  14.6 us
    all_to_all x1, local copies, waits for them, and re-layouts, on_device(): lax.all_to_all(jnp.stack([right_local] * lax.axis_size('rows')), 'rows',...  14.4 us
  transfers between devices with their start and end apart: 2, of which 2 were waited for; matrix products, arithmetic and copies ran while one was open for 2% of the time, Pallas kernels for 0%

profile of v1, /device:TPU:33, one launch (start us, length us, event | category | flops | bytes accessed | tf_op | source)
XLA Modules:
  0.0 385.6 jit_solution(16159264063623407399)
XLA Ops:
  0.0 1.3 convert_reduce_fusion
  1.3 1.4 fusion.12
  2.7 1.4 fusion.14
  4.1 1.0 fusion.10
  5.1 0.2 copy.22
  5.3 0.3 tile.11
  5.6 2.0 reshape.60
  7.6 38.0 %all_to_all.25 = bf16[8,2,16384]{2,1,0:T(2,128)(2,1)} all-to-all(bf16[8,2,16384]{2,1,0:T(2,128)(2,1)S(1)} %reshape.60), channel_id=1, replica_groups=mesh['rows'=64,'cols'=8] {'cols'}, dimensions={0} | all-to-all | bytes 1048576 | tf_op jit(solution)/shard_map/all_to_all | solution.py:44
  45.6 3.1 reshape.61
  48.6 0.0 copy-start.3
  48.7 1.5 bitcast_bitcast_fusion
  50.1 4.5 %reshape.62 = bf16[64,2,2048]{2,1,0:T(2,128)(2,1)} reshape(bf16[1024,8,32]{2,1,0:T(8,128)(2,1)} %bitcast_bitcast_fusion) | data formatting | bytes 1048576
  54.6 15.4 %all-to-all-start.1 = ((bf16[64,2,2048]{2,1,0:T(2,128)(2,1)}), bf16[64,2,2048]{2,1,0:T(2,128)(2,1)S(1)}, u32[]{:S(2)}, u32[]{:S(2)}) async-start(bf16[64,2,2048]{2,1,0:T(2,128)(2,1)} %reshape.62), calls=%async_computation.1 | async-start | bytes 1048576 | tf_op jit(solution)/shard_map/all_to_all | solution.py:43
  70.0 0.2 fusion.11
  70.3 37.2 %all-to-all-done.1 = bf16[64,2,2048]{2,1,0:T(2,128)(2,1)S(1)} async-done(((bf16[64,2,2048]{2,1,0:T(2,128)(2,1)}), bf16[64,2,2048]{2,1,0:T(2,128)(2,1)S(1)}, u32[]{:S(2)}, u32[]{:S(2)}) %all-to-all-start.1) | async-done | bytes 524320 | tf_op jit(solution)/shard_map/all_to_all | solution.py:43
  107.5 2.9 stack.3
  110.4 0.0 copy-done.2
  110.4 5.5 %all-to-all-start.2 = ((bf16[64,8,128,32]{2,3,1,0:T(8,128)(2,1)}), bf16[64,8,128,32]{2,3,1,0:T(8,128)(2,1)}, u32[]{:S(2)}, u32[]{:S(2)}) async-start(bf16[64,8,128,32]{2,3,1,0:T(8,128)(2,1)} %stack.3), calls=%async_computation.2 | async-start | bytes 8388608 | tf_op jit(solution)/shard_map/all_to_all | solution.py:51
  115.9 3.0 reshape.63
  119.0 1.9 copy.24
  120.9 3.1 reshape.56
  124.0 0.1 copy.27
  124.1 175.0 %all-to-all-done.2 = bf16[64,8,128,32]{2,3,1,0:T(8,128)(2,1)} async-done(((bf16[64,8,128,32]{2,3,1,0:T(8,128)(2,1)}), bf16[64,8,128,32]{2,3,1,0:T(8,128)(2,1)}, u32[]{:S(2)}, u32[]{:S(2)}) %all-to-all-start.2) | async-done | bytes 4194336 | tf_op jit(solution)/shard_map/all_to_all | solution.py:51
  299.1 14.4 %copy.26 = bf16[64,8,128,32]{3,2,1,0:T(8,128)(2,1)} copy(bf16[64,8,128,32]{2,3,1,0:T(8,128)(2,1)} %all-to-all-done.2) | data formatting | bytes 8388608 | tf_op jit(solution)/shard_map/all_to_all | solution.py:51
  313.5 21.7 %reshape_reshape.3 = bf16[512,4096]{1,0:T(8,128)(2,1)} reshape(bf16[64,8,128,32]{3,2,1,0:T(8,128)(2,1)} %copy.26) | data formatting | bytes 8388608 | tf_op jit(solution)/shard_map/reshape;reshape | solution.py:58
  335.3 46.3 %while.10 = (s32[]{:T(128)}, f32[4,512,128]{2,1,0:T(8,128)S(1)}, bf16[4,512,128]{2,1,0:T(8,128)(2,1)S(1)}, bf16[512,4096]{1,0:T(8,128)(2,1)}, bf16[1024,128]{1,0:T(8,128)(2,1)S(1)}, /*index=5*/s32[]{:T(128)}) while((s32[]{:T(128)}, f32[4,512,128]{2,1,0:T(8,128)S(1)}, bf16[4,512,128]{2,1,0:T(8,128)(2,1)S(1)}, bf16[512,4096]{1,0:T(8,128)(2,1)}, ...), condition=%wide.region_3.4_spmd, body=%wide.region_2.3_spmd.sunk | while | flops 672137216 | bytes 11141197 | solution.py:80
  335.3 3.0 fusion.36
  338.3 4.4 %reshape.65 = bf16[4,32,128,32]{3,2,1,0:T(8,128)(2,1)} reshape(bf16[128,4096]{1,0:T(8,128)(2,1)S(1)} %fusion.36) | data formatting | bytes 2097152 | tf_op jit(solution)/shard_map/while/body/eval_jaxpr/reshape | solution.py:70
  342.7 3.7 copy.41
  346.4 0.5 fusion.37
  346.9 2.9 fusion.36
  349.9 4.4 %reshape.65 = bf16[4,32,128,32]{3,2,1,0:T(8,128)(2,1)} reshape(bf16[128,4096]{1,0:T(8,128)(2,1)S(1)} %fusion.36) | data formatting | bytes 2097152 | tf_op jit(solution)/shard_map/while/body/eval_jaxpr/reshape | solution.py:70
  354.3 3.7 copy.41
  358.0 0.5 fusion.37
  358.5 2.9 fusion.36
  361.4 4.4 %reshape.65 = bf16[4,32,128,32]{3,2,1,0:T(8,128)(2,1)} reshape(bf16[128,4096]{1,0:T(8,128)(2,1)S(1)} %fusion.36) | data formatting | bytes 2097152 | tf_op jit(solution)/shard_map/while/body/eval_jaxpr/reshape | solution.py:70
  365.9 3.7 copy.41
  369.5 0.5 fusion.37
  370.0 2.9 fusion.36
  373.0 4.4 %reshape.65 = bf16[4,32,128,32]{3,2,1,0:T(8,128)(2,1)} reshape(bf16[128,4096]{1,0:T(8,128)(2,1)S(1)} %fusion.36) | data formatting | bytes 2097152 | tf_op jit(solution)/shard_map/while/body/eval_jaxpr/reshape | solution.py:70
  377.4 3.7 copy.41
  381.1 0.5 fusion.37
  381.6 0.0 copy-start.6
  381.6 0.3 fusion.15
  382.0 0.7 multiply_reduce_fusion
  382.7 0.7 multiply_convert_fusion
  383.4 1.2 fusion.7
  384.7 1.0 add_convert_fusion
  (18 shorter events, 0.1 us)
Async XLA Ops:
  0.0 383.4 %copy-start = (bf16[512,128]{1,0:T(8,128)(2,1)S(1)}, bf16[512,128]{1,0:T(8,128)(2,1)}, u32[]{:S(2)}) copy-start(bf16[512,128]{1,0:T(8,128)(2,1)} %param.19) | copy-start | bytes 393220
  48.6 21.3 %copy-start.3 = (bf16[256,32]{0,1:T(8,128)(2,1)S(1)}, bf16[256,32]{0,1:T(8,128)(2,1)}, u32[]{:S(2)}) copy-start(bf16[256,32]{0,1:T(8,128)(2,1)} %param.15) | copy-start | bytes 49156
  54.6 52.9 %all-to-all-start.1 = ((bf16[64,2,2048]{2,1,0:T(2,128)(2,1)}), bf16[64,2,2048]{2,1,0:T(2,128)(2,1)S(1)}, u32[]{:S(2)}, u32[]{:S(2)}) async-start(bf16[64,2,2048]{2,1,0:T(2,128)(2,1)} %reshape.62), calls=%async_computation.1 | async-start | bytes 1048576 | tf_op jit(solution)/shard_map/all_to_all | solution.py:43
  107.5 3.0 copy-start.2
  110.4 188.7 %all-to-all-start.2 = ((bf16[64,8,128,32]{2,3,1,0:T(8,128)(2,1)}), bf16[64,8,128,32]{2,3,1,0:T(8,128)(2,1)}, u32[]{:S(2)}, u32[]{:S(2)}) async-start(bf16[64,8,128,32]{2,3,1,0:T(8,128)(2,1)} %stack.3), calls=%async_computation.2 | async-start | bytes 8388608 | tf_op jit(solution)/shard_map/all_to_all | solution.py:51
  313.5 21.7 %copy-start.5 = (bf16[1024,128]{1,0:T(8,128)(2,1)S(1)}, bf16[1024,128]{1,0:T(8,128)(2,1)}, u32[]{:S(2)}) copy-start(bf16[1024,128]{1,0:T(8,128)(2,1)} %param.16) | copy-start | bytes 786436
  335.3 46.4 %copy-start.1 = (bf16[16,128,128]{2,1,0:T(8,128)(2,1)S(1)}, bf16[16,128,128]{2,1,0:T(8,128)(2,1)}, u32[]{:S(2)}) copy-start(bf16[16,128,128]{2,1,0:T(8,128)(2,1)} %param.12) | copy-start | bytes 1572868
  335.3 47.4 %copy-start.4 = (f32[128]{0:T(128)S(1)}, f32[128]{0:T(128)}, u32[]{:S(2)}) copy-start(f32[128]{0:T(128)} %param.17) | copy-start | bytes 1540
  381.6 1.8 copy-start.6
